TPU v7x, 256 devices: a whole 4x4x8 slice. The times are simulated.
256 devices in a mesh: gx: 2 (over y_lo), gy: 8 (over x, core), gz: 16 (over z, y_hi).
Axes of the slice: x: 4, y: 4 (y_hi: 2, y_lo: 2; y = y_hi * 2 + y_lo), z: 8, core: 2. Of those that a mesh axis runs over, the one named last changes fastest.
Arguments:
- head_out: bfloat16 [6144, 4096], P(('gy', 'gx'), 'gz'), may hold values from -6 to 6
- out_weight: bfloat16 [4096, 4096], P('gz', ('gx', 'gy')), may hold values from -0.09375 to 0.09375
- residual: bfloat16 [6144, 4096], P(('gy', 'gz'), 'gx'), may hold values from -84 to 84
- norm_gain: bfloat16 [4096], replicated, may hold values from 0.5 to 1.5
Outputs:
- hidden_out: bfloat16 [6144, 4096], P(('gy', 'gz'), 'gx')
- normed: bfloat16 [6144, 4096], P(('gy', 'gz'), 'gx')
All inputs are finite; a program needn't handle non-finite values.
Results may differ from a plain program's by a relative error of at most 0.0098.
Values may be sent and summed in bfloat16 or wider, within the bound.
No kernel may reach another device: no remote copies, remote signals or barrier semaphores. Data moves between devices by JAX's collectives and lax.ppermute only.
A program may use at most 64 MiB of HBM per device.

v0:
```python
import jax
import jax.numpy as jnp
from jax import lax
from jax.sharding import Mesh
from jax.sharding import PartitionSpec as P

GZ = ("gz_0", "gz_1")
GY_GZ = ("gy", "gz_0", "gz_1")


def copy_for_each(value, axis):
    copies = jnp.broadcast_to(value, (lax.axis_size(axis), *value.shape))
    return lax.all_to_all(copies, axis, split_axis=0, concat_axis=0, tiled=True)


def laid_out(tiles, dim):
    lengths = list(tiles.shape[1:])
    lengths[dim] *= tiles.shape[0]
    return jnp.moveaxis(tiles, 0, dim).reshape(lengths)


def collect(value, axis, dim):
    tiles = copy_for_each(value, axis)
    return laid_out(tiles, dim)


def sum_by_axis(terms, axes):
    total = terms.astype(jnp.bfloat16)
    for axis in axes:
        total = lax.psum_scatter(total, axis, scatter_dimension=0, tiled=True)
    return total.astype(jnp.float32)


def of_everyone(value, axis):
    return copy_for_each(value, axis).sum(axis=0)


def shards(head_out, out_weight, residual, norm_gain):
    weight_cols = collect(out_weight, "gy", 1)
    gathered = lax.all_gather(head_out, "gx", axis=0, tiled=True)
    projected = sum_by_axis(jnp.dot(gathered, weight_cols, preferred_element_type=jnp.float32), GZ)
    hidden = (residual.astype(jnp.float32) + projected).astype(jnp.bfloat16)
    gain_all = norm_gain.astype(jnp.float32)
    col_width = hidden.shape[1]
    groups = lax.axis_size("gx")
    widened = lax.optimization_barrier(hidden).astype(jnp.float32)
    squares = of_everyone(jnp.sum(widened * widened, axis=1), "gx")
    inverse = lax.rsqrt(squares / (col_width * groups) + 1e-05)
    gain_slice = lax.dynamic_slice_in_dim(gain_all, lax.axis_index("gx") * col_width, col_width, 0)
    normed = (widened * inverse[:, None] * gain_slice[None, :]).astype(jnp.bfloat16)
    return (hidden, normed)


def solution(mesh):
    split = Mesh(
        mesh.devices.reshape(mesh.shape["gx"], mesh.shape["gy"], 8, 2), ("gx", "gy", "gz_0", "gz_1")
    )
    return jax.shard_map(
        shards,
        mesh=split,
        in_specs=(P(("gy", "gx"), GZ), P(GZ, ("gx", "gy")), P(GY_GZ, "gx"), P()),
        out_specs=(P(GY_GZ, "gx"), P(GY_GZ, "gx")),
        check_vma=False,
    )
```

profile of v0, /device:TPU:2, one launch (start us, length us, event | category | flops | bytes accessed | tf_op | source)
XLA Modules:
  0.0 118.6 jit_solution(8641666479936514836)
XLA Ops:
  7.2 0.0 copy-start.1
  7.2 1.0 copy.8
  8.2 1.0 broadcast_in_dim.8
  9.3 5.7 %all-to-all-start = ((bf16[8,256,256]{1,2,0:T(8,128)(2,1)}), bf16[8,256,256]{1,2,0:T(8,128)(2,1)S(1)}, u32[]{:S(2)}, u32[]{:S(2)}) async-start(bf16[8,256,256]{1,2,0:T(8,128)(2,1)} %broadcast_in_dim.8), calls=%async_computation | async-start | bytes 2097152 | tf_op jit(solution)/shard_map/all_to_all | solution.py:13
  15.0 0.0 reduce-scatter.3.cloned.1.call-start
  15.0 0.0 copy-done.1
  15.0 7.6 %all_gather.3 = bf16[768,256]{1,0:T(8,128)(2,1)S(1)} all-gather(bf16[384,256]{1,0:T(8,128)(2,1)S(1)} %copy-done.1), channel_id=1, replica_groups=mesh['gx'=2,'gy'=8,'gz_0'=8,'gz_1'=2] {'gx'}, dimensions={0}, use_global_device_ids=true | all-gather | bytes 589824 | tf_op jit(solution)/shard_map/all_gather | solution.py:40
  22.6 6.9 %all-to-all-done = bf16[8,256,256]{1,2,0:T(8,128)(2,1)S(1)} async-done(((bf16[8,256,256]{1,2,0:T(8,128)(2,1)}), bf16[8,256,256]{1,2,0:T(8,128)(2,1)S(1)}, u32[]{:S(2)}, u32[]{:S(2)}) %all-to-all-start) | async-done | bytes 1048608 | tf_op jit(solution)/shard_map/all_to_all | solution.py:13
  29.5 0.0 copy-start.2
  29.5 2.7 %convolution_convert_fusion = bf16[768,2048]{1,0:T(8,128)(2,1)} fusion(bf16[768,256]{1,0:T(8,128)(2,1)S(1)} %all_gather.3, bf16[256,2048]{0,1:T(8,128)(2,1)S(1)} %bitcast.6), kind=kOutput, calls=%fused_computation | convolution fusion | flops 806879232 | bytes 4587520 | tf_op jit(solution)/shard_map/dot_general | solution.py:41
  32.1 0.0 copy-start.3
  32.2 0.0 reduce-scatter.3.cloned.1.call-update
  32.2 0.0 reduce-scatter.5.cloned.1.call-start
  32.2 48.2 %reduce-scatter.3.cloned.1.call-done = bf16[96,2048]{1,0:T(8,128)(2,1)} async-done(((bf16[768,2048]{1,0:T(8,128)(2,1)}), bf16[96,2048]{1,0:T(8,128)(2,1)}) %reduce-scatter.3.cloned.1.call-update) | async-done | bytes 393232 | tf_op jit(solution)/shard_map/reduce_scatter | solution.py:30
  80.4 0.0 reduce-scatter.5.cloned.1.call-update
  80.5 21.8 %reduce-scatter.5.cloned.1.call-done = bf16[48,2048]{1,0:T(8,128)(2,1)} async-done(((bf16[96,2048]{1,0:T(8,128)(2,1)}), bf16[48,2048]{1,0:T(8,128)(2,1)}) %reduce-scatter.5.cloned.1.call-update) | async-done | bytes 196624 | tf_op jit(solution)/shard_map/reduce_scatter | solution.py:30
  102.3 0.0 copy-done.2
  102.3 1.0 add_convert_fusion
  103.3 0.0 copy-start
  103.3 0.1 fusion
  103.4 0.6 broadcast_in_dim.9
  104.0 3.2 %all-to-all-start.1 = ((f32[2,1,48]{2,1,0:T(1,128)}), f32[2,1,48]{2,1,0:T(1,128)S(1)}, u32[]{:S(2)}, u32[]{:S(2)}) async-start(f32[2,1,48]{2,1,0:T(1,128)} %broadcast_in_dim.9), calls=%async_computation.3 | async-start | bytes 2048 | tf_op jit(solution)/shard_map/all_to_all | solution.py:13
  107.2 0.0 copy-done.3
  107.2 3.7 %all-to-all-done.1 = f32[2,1,48]{2,1,0:T(1,128)S(1)} async-done(((f32[2,1,48]{2,1,0:T(1,128)}), f32[2,1,48]{2,1,0:T(1,128)S(1)}, u32[]{:S(2)}, u32[]{:S(2)}) %all-to-all-start.1) | async-done | bytes 416 | tf_op jit(solution)/shard_map/all_to_all | solution.py:13
  110.9 0.8 fusion.2
  111.7 0.0 copy-done
  (3 shorter events, 0.0 us)
Async XLA Ops:
  7.2 7.8 %copy-start.1 = (bf16[384,256]{1,0:T(8,128)(2,1)S(1)}, bf16[384,256]{1,0:T(8,128)(2,1)}, u32[]{:S(2)}) copy-start(bf16[384,256]{1,0:T(8,128)(2,1)} %param.4) | copy-start | bytes 589828
  9.3 20.2 %all-to-all-start = ((bf16[8,256,256]{1,2,0:T(8,128)(2,1)}), bf16[8,256,256]{1,2,0:T(8,128)(2,1)S(1)}, u32[]{:S(2)}, u32[]{:S(2)}) async-start(bf16[8,256,256]{1,2,0:T(8,128)(2,1)} %broadcast_in_dim.8), calls=%async_computation | async-start | bytes 2097152 | tf_op jit(solution)/shard_map/all_to_all | solution.py:13
  15.0 65.5 %reduce-scatter.3.cloned.1.call-start = ((), (), s32[]{:S(2)}) async-start(), calls=%async_computation.4 | async-start | bytes 3538944 | tf_op jit(solution)/shard_map/reduce_scatter | solution.py:30
  29.5 72.8 %copy-start.2 = (bf16[48,2048]{1,0:T(8,128)(2,1)S(1)}, bf16[48,2048]{1,0:T(8,128)(2,1)}, u32[]{:S(2)}) copy-start(bf16[48,2048]{1,0:T(8,128)(2,1)} %param.6) | copy-start | bytes 589828
  32.1 75.1 %copy-start.3 = (bf16[4096]{0:T(1024)(128)(2,1)S(1)}, bf16[4096]{0:T(1024)(128)(2,1)}, u32[]{:S(2)}) copy-start(bf16[4096]{0:T(1024)(128)(2,1)} %param.7) | copy-start | bytes 24580
  32.2 70.1 %reduce-scatter.5.cloned.1.call-start = ((), (), s32[]{:S(2)}) async-start(), calls=%async_computation.5 | async-start | bytes 589824 | tf_op jit(solution)/shard_map/reduce_scatter | solution.py:30
  103.3 8.4 %copy-start = (bf16[48,2048]{1,0:T(8,128)(2,1)}, bf16[48,2048]{1,0:T(8,128)(2,1)S(1)}, u32[]{:S(2)}) copy-start(bf16[48,2048]{1,0:T(8,128)(2,1)S(1)} %add_convert_fusion) | copy-start | bytes 589828
  104.0 6.9 %all-to-all-start.1 = ((f32[2,1,48]{2,1,0:T(1,128)}), f32[2,1,48]{2,1,0:T(1,128)S(1)}, u32[]{:S(2)}, u32[]{:S(2)}) async-start(f32[2,1,48]{2,1,0:T(1,128)} %broadcast_in_dim.9), calls=%async_computation.3 | async-start | bytes 2048 | tf_op jit(solution)/shard_map/all_to_all | solution.py:13
Sparse Core Ops, SparseCore 0:
  32.3 48.0 reduce-scatter.2
  82.9 19.3 reduce-scatter.4
where the time goes:
time: 119 us
  waiting for transfers between devices  80.6 us (68%)
  between operations  14.1 us (12%)
  starting transfers between devices  8.94 us (8%)
  blocking collectives  7.59 us (6%)
  local copies, waits for them, and re-layouts  2.67 us (2%)
  matrix products  2.67 us (2%)
  other arithmetic  1.96 us (2%)
    reduce_scatter x2, waiting for transfers between devices, sum_by_axis(): total = lax.psum_scatter(total, axis, scatter_dimension=0, tiled=True)  70 us
    all_to_all x2, waiting for transfers between devices, copy_for_each(): return lax.all_to_all(copies, axis, split_axis=0, concat_axis=0, tiled=True)  10.6 us
    all_to_all x2, starting transfers between devices, copy_for_each(): return lax.all_to_all(copies, axis, split_axis=0, concat_axis=0, tiled=True)  8.9 us
    all_gather x1, blocking collectives, shards(): gathered = lax.all_gather(head_out, 'gx', axis=0, tiled=True)  7.59 us
    dot_general x1, matrix products, shards(): jnp.dot(gathered, weight_cols, preferred_element_type=jnp.float32)  2.67 us
  transfers between devices with their start and end apart: 4, of which 4 were waited for; matrix products, arithmetic and copies ran while one was open for 0% of the time, Pallas kernels for 0%

commit v1 on v0

v1 whole, which is shorter than its diff:
```python
import jax
import jax.numpy as jnp
from jax import lax
from jax.experimental import pallas as pl
from jax.experimental.pallas import tpu as pltpu
from jax.sharding import Mesh
from jax.sharding import PartitionSpec as P

XS, ZS = 4, 8
GY = ("x", "c")
GZ = ("z", "yh")
FLIP = [(0, 1), (1, 0)]
CROSS = [(0, 3), (3, 0), (1, 2), (2, 1)]
BF, F32 = jnp.bfloat16, jnp.float32


def turn(size, step):
    return [(i, (i + step) % size) for i in range(size)]


def shape(*dims, dtype=BF):
    return jax.ShapeDtypeStruct(dims, dtype)


def call(body, outs, where, *args, scratch=()):
    smem = pl.BlockSpec(memory_space=pltpu.SMEM)
    vmem = pl.BlockSpec(memory_space=pltpu.VMEM)
    return pl.pallas_call(
        body,
        out_shape=outs,
        in_specs=[smem] + [vmem] * len(args),
        out_specs=jax.tree.map(lambda _: vmem, outs),
        scratch_shapes=scratch,
    )(where, *args)


def pack(where, heads, weights, mine, theirs, both):
    yh = where[3]
    part = mine.shape[0] // 4
    for block in range(4):
        to = pl.ds(block * part, part)
        own = pl.ds(pl.multiple_of((2 * block + yh) * part, part), part)
        other = pl.ds(pl.multiple_of((2 * block + 1 - yh) * part, part), part)
        mine[to, :] = heads[own, :]
        theirs[to, :] = heads[other, :]
        both[to, :] = heads[other, :]
    both[4 * part :, :] = weights[...]


def multiply(where, mine, side, cross, both, *refs):
    tiles, (zero, p1, m1, p2, m2, p3, m3, p4, m4, rows) = refs[: 4 * XS], refs[4 * XS :]
    part, depth = mine.shape[0] // 4, mine.shape[1]
    half = XS * tiles[0].shape[1]
    first = where[1]
    for source, near, far in ((0, mine, both), (1, side, cross)):
        for block in range(4):
            at = lax.rem(source * 4 + block + first, ZS)
            to = pl.ds(pl.multiple_of(at * part, part), part)
            rows[to, :depth] = near[block * part : (block + 1) * part, :]
            rows[to, depth:] = far[block * part : (block + 1) * part, :]
    left, right = rows[:, :depth], rows[:, depth:]
    width = tiles[0].shape[1]
    for t in range(2 * XS):
        out = jnp.dot(left, tiles[2 * t][...], preferred_element_type=F32)
        out += jnp.dot(right, tiles[2 * t + 1][...], preferred_element_type=F32)
        col = slice(t * width, (t + 1) * width)
        piece = [out[k * part : (k + 1) * part, :] for k in range(ZS)]
        zero[:, col] = piece[0]
        p1[:, col] = piece[1].astype(BF)
        p2[:, col] = piece[2]
        p3[:, col] = piece[3].astype(BF)
        m3[:, col] = piece[5].astype(BF)
        m2[:, col] = piece[6]
        m1[:, col] = piece[7].astype(BF)
        if t < XS:
            p4[:, col] = piece[4].astype(BF)
        else:
            m4[:, t * width - half : (t + 1) * width - half] = piece[4].astype(BF)


def relay(where, p2, m2, p3, m3, p4, m4, up, down):
    half = p4.shape[1]
    up[:, :half] = (p2[:, :half] + p3[:, :half].astype(F32) + p4[...].astype(F32)).astype(BF)
    up[:, half:] = (p2[:, half:] + p3[:, half:].astype(F32)).astype(BF)
    down[:, :half] = (m2[:, :half] + m3[:, :half].astype(F32)).astype(BF)
    down[:, half:] = (m2[:, half:] + m3[:, half:].astype(F32) + m4[...].astype(F32)).astype(BF)


def finish(where, zero, p1, m1, up, down, residual, hidden, squares):
    x, c = where[0], where[4]
    width = residual.shape[1] // (2 * XS)
    total = jnp.zeros(squares.shape, F32)
    for t in range(2 * XS):
        col = slice(t * width, (t + 1) * width)
        block = lax.rem(x + t // 2, XS) * 2 + lax.rem(c + t % 2, 2)
        to = pl.ds(pl.multiple_of(block * width, width), width)
        projected = zero[:, col]
        for ref in (p1, m1, up, down):
            projected += ref[:, col].astype(F32)
        out = (residual[:, to].astype(F32) + projected).astype(BF)
        hidden[:, to] = out
        wide = out.astype(F32)
        for lane in range(0, width, 128):
            total += wide[:, lane : lane + 128] * wide[:, lane : lane + 128]
    squares[...] = total


def normalize(where, hidden, near, far, gain, normed):
    width = hidden.shape[1]
    squares = jnp.sum(near[...] + far[...], axis=1, keepdims=True)
    inverse = lax.rsqrt(squares / (2 * width) + 1e-05)
    mine = gain[:, pl.ds(pl.multiple_of(where[2] * width, width), width)].astype(F32)
    normed[...] = (hidden[...].astype(F32) * inverse * mine).astype(BF)


def shards(head_out, out_weight, residual, norm_gain):
    x, z, yh, gx, c = (lax.axis_index(name) for name in ("x", "z", "yh", "gx", "c"))
    where = jnp.stack([x, (gx * 4 - z + ZS) % ZS, gx, yh, c]).astype(jnp.int32)
    rows, depth = head_out.shape
    cols = out_weight.shape[1]
    part = rows // 8
    width = 2 * XS * cols
    half = shape(rows // 2, depth)
    mine, theirs, both = call(
        pack, (half, half, shape(rows // 2 + depth, depth)), where, head_out, out_weight
    )
    both = lax.ppermute(both, "yh", FLIP)
    side = lax.ppermute(mine, "gx", FLIP)
    cross = lax.ppermute(theirs, ("gx", "yh"), CROSS)
    far_weight = both[rows // 2 :]
    tiles = []
    for k in range(XS):
        own = lax.ppermute(out_weight, "x", turn(XS, -k)) if k else out_weight
        far = lax.ppermute(far_weight, "x", turn(XS, -k)) if k else far_weight
        tiles += [own, far, lax.ppermute(own, "c", FLIP), lax.ppermute(far, "c", FLIP)]
    full, narrow = shape(part, width), shape(part, width // 2)
    wide = shape(part, width, dtype=F32)
    zero, p1, m1, p2, m2, p3, m3, p4, m4 = call(
        multiply,
        (wide, full, full, wide, wide, full, full, narrow, narrow),
        where, mine, side, cross, both, *tiles,
        scratch=[pltpu.VMEM((rows, 2 * depth), BF)],
    )
    p4, m4 = lax.ppermute(p4, "z", turn(ZS, 2)), lax.ppermute(m4, "z", turn(ZS, -2))
    p3, m3 = lax.ppermute(p3, "z", turn(ZS, 1)), lax.ppermute(m3, "z", turn(ZS, -1))
    p1, m1 = lax.ppermute(p1, "z", turn(ZS, 1)), lax.ppermute(m1, "z", turn(ZS, -1))
    up, down = call(relay, (full, full), where, p2, m2, p3, m3, p4, m4)
    up, down = lax.ppermute(up, "z", turn(ZS, 2)), lax.ppermute(down, "z", turn(ZS, -2))
    hidden, squares = call(
        finish, (full, shape(part, 128, dtype=F32)), where, zero, p1, m1, up, down, residual
    )
    others = lax.ppermute(squares, "gx", FLIP)
    gain = norm_gain.reshape(1, -1)
    normed = call(normalize, full, where, hidden, squares, others, gain)
    return (hidden, normed)


def solution(mesh):
    split = Mesh(mesh.devices.reshape(2, XS, 2, ZS, 2), ("gx", *GY, *GZ))
    return jax.shard_map(
        shards,
        mesh=split,
        in_specs=(P((*GY, "gx"), GZ), P(GZ, ("gx", *GY)), P((*GY, *GZ), "gx"), P()),
        out_specs=(P((*GY, *GZ), "gx"), P((*GY, *GZ), "gx")),
        check_vma=False,
    )
```

time: 119 us -> 79.3 us (0.67)
  waiting for transfers between devices: 80.6 us -> 30.7 us
  starting transfers between devices: 8.94 us -> 31.2 us
  between operations: 14.1 us -> 0.98 us
  Pallas kernels: 0 us -> 11.9 us
  blocking collectives: 7.59 us -> 0 us
  matrix products: 2.67 us -> 0 us
  other arithmetic: 1.96 us -> 0 us
  local copies, waits for them, and re-layouts: 2.67 us -> 4.32 us
    reduce_scatter x2 -> x0, waiting for transfers between devices: 70 us -> none  [sum_by_axis(): total = lax.psum_scatter(total, axis, scatter_dimension=0, tiled=True)]
    ppermute x0 -> x26, starting transfers between devices: none -> 31.2 us  [the longest x1 4.21 us: shards(): lax.ppermute(m3, 'z', turn(ZS, -1))]
    ppermute x0 -> x26, waiting for transfers between devices: none -> 30.7 us  [the longest x1 6.96 us: shards(): lax.ppermute(p4, 'z', turn(ZS, 2))]
    pallas_call x0 -> x5, Pallas kernels: none -> 11.9 us  [call(): pl.pallas_call(body, out_shape=outs, in_specs=[smem] + [vmem] * len(args)...]
    all_to_all x2 -> x0, waiting for transfers between devices: 10.6 us -> none  [copy_for_each(): return lax.all_to_all(copies, axis, split_axis=0, concat_axis=0, tiled=True)]
    all_to_all x2 -> x0, starting transfers between devices: 8.9 us -> none  [copy_for_each(): return lax.all_to_all(copies, axis, split_axis=0, concat_axis=0, tiled=True)]
    all_gather x1 -> x0, blocking collectives: 7.59 us -> none  [shards(): gathered = lax.all_gather(head_out, 'gx', axis=0, tiled=True)]
    dot_general x1 -> x0, matrix products: 2.67 us -> none  [shards(): jnp.dot(gathered, weight_cols, preferred_element_type=jnp.float32)]
  transfers between devices with their start and end apart: 4 -> 26, of which waited for: 4 -> 10; matrix products, arithmetic and copies ran while one was open for 0% -> 1% of each run, Pallas kernels for 0% -> 3%
where the time goes in v1:
time: 79.3 us; the launch traced here: 79.1 us
  starting transfers between devices  31.2 us (39%)
  waiting for transfers between devices  30.7 us (39%)
  Pallas kernels  11.9 us (15%)
  local copies, waits for them, and re-layouts  4.32 us (5%)
  between operations  0.98 us (1%)
    pallas_call x5, Pallas kernels, call(): pl.pallas_call(body, out_shape=outs, in_specs=[smem] + [vmem] * len(args)...  11.9 us
    ppermute x1, waiting for transfers between devices, shards(): lax.ppermute(p4, 'z', turn(ZS, 2))  6.96 us
    ppermute x1, waiting for transfers between devices, shards(): lax.ppermute(up, 'z', turn(ZS, 2))  5.74 us
    ppermute x3, waiting for transfers between devices, shards(): far = lax.ppermute(far_weight, 'x', turn(XS, -k)) if k else far_weight  4.65 us
    ppermute x1, waiting for transfers between devices, shards(): cross = lax.ppermute(theirs, ('gx', 'yh'), CROSS)  4.37 us
    ppermute x1, starting transfers between devices, shards(): lax.ppermute(m3, 'z', turn(ZS, -1))  4.21 us
    ppermute x3, starting transfers between devices, shards(): own = lax.ppermute(out_weight, 'x', turn(XS, -k)) if k else out_weight  4.15 us
    ppermute x3, starting transfers between devices, shards(): far = lax.ppermute(far_weight, 'x', turn(XS, -k)) if k else far_weight  4.13 us
  transfers between devices with their start and end apart: 26, of which 10 were waited for; matrix products, arithmetic and copies ran while one was open for 1% of the time, Pallas kernels for 3%

profile of v1, /device:TPU:2, one launch (start us, length us, event | category | flops | bytes accessed | tf_op | source)
XLA Modules:
  0.0 79.1 jit_solution(6382006114656305948)
XLA Ops:
  0.6 0.6 stack.23.where
  1.3 1.8 %shard_map.59 = (bf16[192,256]{1,0:T(8,128)(2,1)}, bf16[192,256]{1,0:T(8,128)(2,1)}, bf16[448,256]{1,0:T(8,128)(2,1)}) custom-call(s32[5]{0:T(128)} %stack.23.where, bf16[384,256]{1,0:T(8,128)(2,1)} %heads.1, bf16[256,256]{1,0:T(8,128)(2,1)} %refs_0_.1), custom_call_target="tpu_custom_call" | custom-call | tf_op jit(solution)/shard_map/pallas_call | solution.py:28
  3.1 3.2 %collective-permute-start.2 = (bf16[448,256]{1,0:T(8,128)(2,1)}, bf16[448,256]{1,0:T(8,128)(2,1)S(1)}, u32[]{:S(2)}, u32[]{:S(2)}) collective-permute-start(bf16[448,256]{1,0:T(8,128)(2,1)} %get-tuple-element.20), channel_id=1, source_target_pairs={{0,1},{1,0},{2,3},{3,2},{4,5},{5,4},{6,7},{7,6},{8,9},{9,8},{10,11... | collective-permute-start | bytes 688136 | tf_op jit(solution)/shard_map/ppermute | solution.py:127
  6.3 0.7 collective-permute-start
  7.0 2.1 %collective-permute-start.9 = (bf16[256,256]{1,0:T(8,128)(2,1)S(1)}, bf16[256,256]{1,0:T(8,128)(2,1)S(1)}, u32[]{:S(2)}, u32[]{:S(2)}) collective-permute-start(bf16[256,256]{1,0:T(8,128)(2,1)S(1)} %copy-done.1), channel_id=1, source_target_pairs={{0,64},{32,96},{64,0},{96,32},{1,65},{33,97},{65,1},{97,33},{2,66}... | collective-permute-start | bytes 393224 | tf_op jit(solution)/shard_map/ppermute | solution.py:133
  9.1 0.0 collective-permute-start.13
  9.1 2.0 %collective-permute-start.5 = (bf16[256,256]{1,0:T(8,128)(2,1)S(1)}, bf16[256,256]{1,0:T(8,128)(2,1)S(1)}, u32[]{:S(2)}, u32[]{:S(2)}) collective-permute-start(bf16[256,256]{1,0:T(8,128)(2,1)S(1)} %copy-done.1), channel_id=1, source_target_pairs={{0,96},{32,0},{64,32},{96,64},{1,97},{33,1},{65,33},{97,65},{2,98}... | collective-permute-start | bytes 393224 | tf_op jit(solution)/shard_map/ppermute | solution.py:133
  11.1 3.5 %collective-permute-done.side = bf16[192,256]{1,0:T(8,128)(2,1)S(1)} collective-permute-done((bf16[192,256]{1,0:T(8,128)(2,1)}, bf16[192,256]{1,0:T(8,128)(2,1)S(1)}, u32[]{:S(2)}, u32[]{:S(2)}) %collective-permute-start) | collective-permute-done | bytes 98336 | tf_op jit(solution)/shard_map/ppermute | solution.py:128
  14.6 0.0 collective-permute-start.3
  14.6 0.0 collective-permute-done.2.both
  14.6 1.6 %collective-permute-start.1 = (bf16[192,256]{1,0:T(8,128)(2,1)}, bf16[192,256]{1,0:T(8,128)(2,1)S(1)}, u32[]{:S(2)}, u32[]{:S(2)}) collective-permute-start(bf16[192,256]{1,0:T(8,128)(2,1)} %get-tuple-element.19), channel_id=1, source_target_pairs={{0,129},{129,0},{1,128},{128,1},{2,131},{131,2},{3,130},{130,3},{4... | collective-permute-start | bytes 294920 | tf_op jit(solution)/shard_map/ppermute | solution.py:129
  16.2 0.0 collective-permute-done.9.refs_8_
  16.3 0.1 collective-permute-start.11
  16.4 0.0 collective-permute-done.13.refs_12_
  16.4 0.5 collective-permute-start.15
  16.9 4.4 %collective-permute-done.1.cross = bf16[192,256]{1,0:T(8,128)(2,1)S(1)} collective-permute-done((bf16[192,256]{1,0:T(8,128)(2,1)}, bf16[192,256]{1,0:T(8,128)(2,1)S(1)}, u32[]{:S(2)}, u32[]{:S(2)}) %collective-permute-start.1) | collective-permute-done | bytes 98336 | tf_op jit(solution)/shard_map/ppermute | solution.py:129
  21.2 2.1 %collective-permute-start.10 = (bf16[256,256]{1,0:T(8,128)(2,1)S(1)}, bf16[256,256]{1,0:T(8,128)(2,1)S(1)}, u32[]{:S(2)}, u32[]{:S(2)}) collective-permute-start(bf16[256,256]{1,0:T(8,128)(2,1)S(1)} %slice.4.refs_1_), channel_id=1, source_target_pairs={{0,64},{32,96},{64,0},{96,32},{1,65},{33,97},{65,1},{97,33},{2,66}... | collective-permute-start | bytes 393224 | tf_op jit(solution)/shard_map/ppermute | solution.py:134
  23.4 0.0 collective-permute-done.5.refs_4_
  23.4 0.0 collective-permute-start.14
  23.4 0.0 collective-permute-done.3.refs_2_
  23.4 2.0 %collective-permute-start.6 = (bf16[256,256]{1,0:T(8,128)(2,1)S(1)}, bf16[256,256]{1,0:T(8,128)(2,1)S(1)}, u32[]{:S(2)}, u32[]{:S(2)}) collective-permute-start(bf16[256,256]{1,0:T(8,128)(2,1)S(1)} %slice.4.refs_1_), channel_id=1, source_target_pairs={{0,96},{32,0},{64,32},{96,64},{1,97},{33,1},{65,33},{97,65},{2,98}... | collective-permute-start | bytes 393224 | tf_op jit(solution)/shard_map/ppermute | solution.py:134
  25.4 0.0 collective-permute-done.11.refs_10_
  25.4 0.0 collective-permute-start.7
  25.4 0.0 collective-permute-done.15.refs_14_
  25.4 0.5 collective-permute-start.4
  25.9 2.8 %collective-permute-done.10.refs_9_ = bf16[256,256]{1,0:T(8,128)(2,1)S(1)} collective-permute-done((bf16[256,256]{1,0:T(8,128)(2,1)S(1)}, bf16[256,256]{1,0:T(8,128)(2,1)S(1)}, u32[]{:S(2)}, u32[]{:S(2)}) %collective-permute-start.10) | collective-permute-done | bytes 131104 | tf_op jit(solution)/shard_map/ppermute | solution.py:134
  28.7 0.0 collective-permute-start.12
  28.7 1.9 %collective-permute-done.14.refs_13_ = bf16[256,256]{1,0:T(8,128)(2,1)S(1)} collective-permute-done((bf16[256,256]{1,0:T(8,128)(2,1)S(1)}, bf16[256,256]{1,0:T(8,128)(2,1)S(1)}, u32[]{:S(2)}, u32[]{:S(2)}) %collective-permute-start.14) | collective-permute-done | bytes 131104 | tf_op jit(solution)/shard_map/ppermute | solution.py:134
  30.6 0.0 collective-permute-start.16
  30.6 0.0 collective-permute-done.6.refs_5_
  30.6 0.5 collective-permute-start.8
  31.1 0.0 collective-permute-done.7.refs_6_
  31.1 0.0 collective-permute-done.4.refs_3_
  31.1 0.0 collective-permute-done.12.refs_11_
  31.2 0.8 collective-permute-done.16.refs_15_
  31.9 0.2 collective-permute-done.8.refs_7_
  32.3 0.3 copy-done.21
  32.6 0.7 copy-done.22
  33.2 4.0 %shard_map.60 = (f32[48,2048]{1,0:T(8,128)}, bf16[48,2048]{1,0:T(8,128)(2,1)}, bf16[48,2048]{1,0:T(8,128)(2,1)}, f32[48,2048]{1,0:T(8,128)}, f32[48,2048]{1,0:T(...) custom-call(s32[5]{0:T(128)} %stack.23.where, ...), custom_call_target="tpu_custom_call" | custom-call | tf_op jit(solution)/shard_map/pallas_call | solution.py:28
  37.2 2.0 %collective-permute-start.19 = (bf16[48,2048]{1,0:T(8,128)(2,1)}, bf16[48,2048]{1,0:T(8,128)(2,1)S(1)}, u32[]{:S(2)}, u32[]{:S(2)}) collective-permute-start(bf16[48,2048]{1,0:T(8,128)(2,1)} %get-tuple-element.26), channel_id=1, source_target_pairs={{0,2},{2,4},{4,6},{6,8},{8,10},{10,12},{12,14},{14,0},{1,3},{3,5},... | collective-permute-start | bytes 589832 | tf_op jit(solution)/shard_map/ppermute | solution.py:145
  39.2 4.2 %collective-permute-start.20 = (bf16[48,2048]{1,0:T(8,128)(2,1)}, bf16[48,2048]{1,0:T(8,128)(2,1)S(1)}, u32[]{:S(2)}, u32[]{:S(2)}) collective-permute-start(bf16[48,2048]{1,0:T(8,128)(2,1)} %get-tuple-element.27), channel_id=1, source_target_pairs={{0,14},{2,0},{4,2},{6,4},{8,6},{10,8},{12,10},{14,12},{1,15},{3,1}... | collective-permute-start | bytes 589832 | tf_op jit(solution)/shard_map/ppermute | solution.py:145
  43.4 0.0 collective-permute-start.21
  43.4 4.1 %collective-permute-start.22 = (bf16[48,1024]{1,0:T(8,128)(2,1)}, bf16[48,1024]{1,0:T(8,128)(2,1)S(1)}, u32[]{:S(2)}, u32[]{:S(2)}) collective-permute-start(bf16[48,1024]{1,0:T(8,128)(2,1)} %get-tuple-element.29), channel_id=1, source_target_pairs={{0,12},{2,14},{4,0},{6,2},{8,4},{10,6},{12,8},{14,10},{1,13},{3,15... | collective-permute-start | bytes 294920 | tf_op jit(solution)/shard_map/ppermute | solution.py:144
  47.6 0.0 collective-permute-start.17
  47.6 7.0 %collective-permute-done.21.p4 = bf16[48,1024]{1,0:T(8,128)(2,1)S(1)} collective-permute-done((bf16[48,1024]{1,0:T(8,128)(2,1)}, bf16[48,1024]{1,0:T(8,128)(2,1)S(1)}, u32[]{:S(2)}, u32[]{:S(2)}) %collective-permute-start.21) | collective-permute-done | bytes 98336 | tf_op jit(solution)/shard_map/ppermute | solution.py:144
  54.5 1.3 %collective-permute-start.18 = (bf16[48,2048]{1,0:T(8,128)(2,1)}, bf16[48,2048]{1,0:T(8,128)(2,1)S(1)}, u32[]{:S(2)}, u32[]{:S(2)}) collective-permute-start(bf16[48,2048]{1,0:T(8,128)(2,1)} %get-tuple-element.23), channel_id=1, source_target_pairs={{0,14},{2,0},{4,2},{6,4},{8,6},{10,8},{12,10},{14,12},{1,15},{3,1}... | collective-permute-start | bytes 589832 | tf_op jit(solution)/shard_map/ppermute | solution.py:146
  55.8 0.0 collective-permute-done.22.m4
  55.8 0.0 collective-permute-done.19.p3
  55.9 0.6 copy-done.26
  56.5 0.1 copy-done.5
  56.5 0.1 copy-done.6
  56.6 2.1 %shard_map.61 = (bf16[48,2048]{1,0:T(8,128)(2,1)}, bf16[48,2048]{1,0:T(8,128)(2,1)}) custom-call(s32[5]{0:T(128)} %stack.23.where, f32[48,2048]{1,0:T(8,128)} %get-tuple-element.24.p2, f32[48,2048]{1,0:T(8,128)} %get-tuple-element.25.m2, bf16[48,2048]{1,0:T(8,128)(2,1)} %copy-done.5, bf16[48,2048]{1,0:T(8,128)(2,1)} %copy-done.6, ...), custom_call_target="tpu_custom_call" | custom-call | tf_op jit(solution)/shard_map/pallas_call | solution.py:28
  58.7 1.7 %collective-permute-start.23 = (bf16[48,2048]{1,0:T(8,128)(2,1)}, bf16[48,2048]{1,0:T(8,128)(2,1)S(1)}, u32[]{:S(2)}, u32[]{:S(2)}) collective-permute-start(bf16[48,2048]{1,0:T(8,128)(2,1)} %get-tuple-element.30), channel_id=1, source_target_pairs={{0,4},{2,6},{4,8},{6,10},{8,12},{10,14},{12,0},{14,2},{1,5},{3,7},... | collective-permute-start | bytes 589832 | tf_op jit(solution)/shard_map/ppermute | solution.py:148
  60.4 2.5 %collective-permute-start.24 = (bf16[48,2048]{1,0:T(8,128)(2,1)}, bf16[48,2048]{1,0:T(8,128)(2,1)S(1)}, u32[]{:S(2)}, u32[]{:S(2)}) collective-permute-start(bf16[48,2048]{1,0:T(8,128)(2,1)} %get-tuple-element.31), channel_id=1, source_target_pairs={{0,12},{2,14},{4,0},{6,2},{8,4},{10,6},{12,8},{14,10},{1,13},{3,15... | collective-permute-start | bytes 589832 | tf_op jit(solution)/shard_map/ppermute | solution.py:148
  62.9 0.0 collective-permute-done.18.m1
  62.9 5.7 %collective-permute-done.23.up = bf16[48,2048]{1,0:T(8,128)(2,1)S(1)} collective-permute-done((bf16[48,2048]{1,0:T(8,128)(2,1)}, bf16[48,2048]{1,0:T(8,128)(2,1)S(1)}, u32[]{:S(2)}, u32[]{:S(2)}) %collective-permute-start.23) | collective-permute-done | bytes 196640 | tf_op jit(solution)/shard_map/ppermute | solution.py:148
  68.6 1.2 %collective-permute-done.24.down = bf16[48,2048]{1,0:T(8,128)(2,1)S(1)} collective-permute-done((bf16[48,2048]{1,0:T(8,128)(2,1)}, bf16[48,2048]{1,0:T(8,128)(2,1)S(1)}, u32[]{:S(2)}, u32[]{:S(2)}) %collective-permute-start.24) | collective-permute-done | bytes 196640 | tf_op jit(solution)/shard_map/ppermute | solution.py:148
  69.8 0.7 copy-done.8
  70.5 2.2 %shard_map.62 = (bf16[48,2048]{1,0:T(8,128)(2,1)}, f32[48,128]{1,0:T(8,128)}) custom-call(s32[5]{0:T(128)} %stack.23.where, f32[48,2048]{1,0:T(8,128)} %get-tuple-element.21.zero, bf16[48,2048]{1,0:T(8,128)(2,1)} %copy-done.3, bf16[48,2048]{1,0:T(8,128)(2,1)} %copy-done.4, bf16[48,2048]{1,0:T(8,128)(2,1)} %copy-done.7, bf16[48,2048]{1,0:T(8,128)(2,1)} %copy-done.8, ...), custom_call_target="tpu_custom_call" | custom-call | tf_op jit(solution)/shard_map/pallas_call | solution.py:28
  72.7 0.1 collective-permute-start.25
  72.8 0.6 reshape.7.gain
  73.4 3.3 %collective-permute-done.25.far = f32[48,128]{1,0:T(8,128)S(1)} collective-permute-done((f32[48,128]{1,0:T(8,128)}, f32[48,128]{1,0:T(8,128)S(1)}, u32[]{:S(2)}, u32[]{:S(2)}) %collective-permute-start.25) | collective-permute-done | bytes 24608 | tf_op jit(solution)/shard_map/ppermute | solution.py:152
  76.7 0.6 copy-done.27
  77.3 1.8 %shard_map.63 = bf16[48,2048]{1,0:T(8,128)(2,1)} custom-call(s32[5]{0:T(128)} %stack.23.where, bf16[48,2048]{1,0:T(8,128)(2,1)} %get-tuple-element.16.hidden, f32[48,128]{1,0:T(8,128)} %get-tuple-element.33.near, f32[48,128]{1,0:T(8,128)} %copy-done.27, bf16[1,4096]{1,0:T(2,128)(2,1)} %reshape.7.gain), custom_call_target="tpu_custom_call" | custom-call | tf_op jit(solution)/shard_map/pallas_call | solution.py:28
  (54 shorter events, 0.1 us)
Async XLA Ops:
  1.3 5.7 %copy-start.1 = (bf16[256,256]{1,0:T(8,128)(2,1)S(1)}, bf16[256,256]{1,0:T(8,128)(2,1)}, u32[]{:S(2)}) copy-start(bf16[256,256]{1,0:T(8,128)(2,1)} %refs_0_.1) | copy-start | bytes 393220
  3.1 11.5 %collective-permute-start.2 = (bf16[448,256]{1,0:T(8,128)(2,1)}, bf16[448,256]{1,0:T(8,128)(2,1)S(1)}, u32[]{:S(2)}, u32[]{:S(2)}) collective-permute-start(bf16[448,256]{1,0:T(8,128)(2,1)} %get-tuple-element.20), channel_id=1, source_target_pairs={{0,1},{1,0},{2,3},{3,2},{4,5},{5,4},{6,7},{7,6},{8,9},{9,8},{10,11... | collective-permute-start | bytes 688136 | tf_op jit(solution)/shard_map/ppermute | solution.py:127
  6.3 8.3 %collective-permute-start = (bf16[192,256]{1,0:T(8,128)(2,1)}, bf16[192,256]{1,0:T(8,128)(2,1)S(1)}, u32[]{:S(2)}, u32[]{:S(2)}) collective-permute-start(bf16[192,256]{1,0:T(8,128)(2,1)} %get-tuple-element.18.mine), channel_id=1, source_target_pairs={{0,128},{128,0},{1,129},{129,1},{2,130},{130,2},{3,131},{131,3},{4... | collective-permute-start | bytes 294920 | tf_op jit(solution)/shard_map/ppermute | solution.py:128
  7.0 9.3 %collective-permute-start.9 = (bf16[256,256]{1,0:T(8,128)(2,1)S(1)}, bf16[256,256]{1,0:T(8,128)(2,1)S(1)}, u32[]{:S(2)}, u32[]{:S(2)}) collective-permute-start(bf16[256,256]{1,0:T(8,128)(2,1)S(1)} %copy-done.1), channel_id=1, source_target_pairs={{0,64},{32,96},{64,0},{96,32},{1,65},{33,97},{65,1},{97,33},{2,66}... | collective-permute-start | bytes 393224 | tf_op jit(solution)/shard_map/ppermute | solution.py:133
  9.1 7.3 %collective-permute-start.13 = (bf16[256,256]{1,0:T(8,128)(2,1)S(1)}, bf16[256,256]{1,0:T(8,128)(2,1)S(1)}, u32[]{:S(2)}, u32[]{:S(2)}) collective-permute-start(bf16[256,256]{1,0:T(8,128)(2,1)S(1)} %copy-done.1), channel_id=1, source_target_pairs={{0,32},{32,64},{64,96},{96,0},{1,33},{33,65},{65,97},{97,1},{2,34}... | collective-permute-start | bytes 393224 | tf_op jit(solution)/shard_map/ppermute | solution.py:133
  9.1 14.3 %collective-permute-start.5 = (bf16[256,256]{1,0:T(8,128)(2,1)S(1)}, bf16[256,256]{1,0:T(8,128)(2,1)S(1)}, u32[]{:S(2)}, u32[]{:S(2)}) collective-permute-start(bf16[256,256]{1,0:T(8,128)(2,1)S(1)} %copy-done.1), channel_id=1, source_target_pairs={{0,96},{32,0},{64,32},{96,64},{1,97},{33,1},{65,33},{97,65},{2,98}... | collective-permute-start | bytes 393224 | tf_op jit(solution)/shard_map/ppermute | solution.py:133
  14.6 17.5 %copy-start.23 = (bf16[192,256]{1,0:T(8,128)(2,1)}, bf16[192,256]{1,0:T(8,128)(2,1)S(1)}, u32[]{:S(2)}) copy-start(bf16[192,256]{1,0:T(8,128)(2,1)S(1)} %collective-permute-done.side) | copy-start | bytes 294916
  14.6 8.8 %collective-permute-start.3 = (bf16[256,256]{1,0:T(8,128)(2,1)S(1)}, bf16[256,256]{1,0:T(8,128)(2,1)S(1)}, u32[]{:S(2)}, u32[]{:S(2)}) collective-permute-start(bf16[256,256]{1,0:T(8,128)(2,1)S(1)} %copy-done.1), channel_id=1, source_target_pairs={{0,16},{16,0},{1,17},{17,1},{2,18},{18,2},{3,19},{19,3},{4,20},{20... | collective-permute-start | bytes 393224 | tf_op jit(solution)/shard_map/ppermute | solution.py:135
  14.6 17.5 %copy-start = (bf16[448,256]{1,0:T(8,128)(2,1)}, bf16[448,256]{1,0:T(8,128)(2,1)S(1)}, u32[]{:S(2)}) copy-start(bf16[448,256]{1,0:T(8,128)(2,1)S(1)} %collective-permute-done.2.both) | copy-start | bytes 688132
  14.6 6.6 %collective-permute-start.1 = (bf16[192,256]{1,0:T(8,128)(2,1)}, bf16[192,256]{1,0:T(8,128)(2,1)S(1)}, u32[]{:S(2)}, u32[]{:S(2)}) collective-permute-start(bf16[192,256]{1,0:T(8,128)(2,1)} %get-tuple-element.19), channel_id=1, source_target_pairs={{0,129},{129,0},{1,128},{128,1},{2,131},{131,2},{3,130},{130,3},{4... | collective-permute-start | bytes 294920 | tf_op jit(solution)/shard_map/ppermute | solution.py:129
  16.2 15.9 %copy-start.2 = (bf16[256,256]{1,0:T(8,128)(2,1)}, bf16[256,256]{1,0:T(8,128)(2,1)S(1)}, u32[]{:S(2)}) copy-start(bf16[256,256]{1,0:T(8,128)(2,1)S(1)} %slice.4.refs_1_) | copy-start | bytes 393220
  16.3 15.9 %copy-start.9 = (bf16[256,256]{1,0:T(8,128)(2,1)}, bf16[256,256]{1,0:T(8,128)(2,1)S(1)}, u32[]{:S(2)}) copy-start(bf16[256,256]{1,0:T(8,128)(2,1)S(1)} %collective-permute-done.9.refs_8_) | copy-start | bytes 393220
  16.3 9.1 %collective-permute-start.11 = (bf16[256,256]{1,0:T(8,128)(2,1)S(1)}, bf16[256,256]{1,0:T(8,128)(2,1)S(1)}, u32[]{:S(2)}, u32[]{:S(2)}) collective-permute-start(bf16[256,256]{1,0:T(8,128)(2,1)S(1)} %collective-permute-done.9.refs_8_), channel_id=1, source_target_pairs={{0,16},{16,0},{1,17},{17,1},{2,18},{18,2},{3,19},{19,3},{4,20},{20... | collective-permute-start | bytes 393224 | tf_op jit(solution)/shard_map/ppermute | solution.py:135
  16.4 15.8 %copy-start.10 = (bf16[256,256]{1,0:T(8,128)(2,1)}, bf16[256,256]{1,0:T(8,128)(2,1)S(1)}, u32[]{:S(2)}) copy-start(bf16[256,256]{1,0:T(8,128)(2,1)S(1)} %collective-permute-done.13.refs_12_) | copy-start | bytes 393220
  16.4 9.0 %collective-permute-start.15 = (bf16[256,256]{1,0:T(8,128)(2,1)S(1)}, bf16[256,256]{1,0:T(8,128)(2,1)S(1)}, u32[]{:S(2)}, u32[]{:S(2)}) collective-permute-start(bf16[256,256]{1,0:T(8,128)(2,1)S(1)} %collective-permute-done.13.refs_12_), channel_id=1, source_target_pairs={{0,16},{16,0},{1,17},{17,1},{2,18},{18,2},{3,19},{19,3},{4,20},{20... | collective-permute-start | bytes 393224 | tf_op jit(solution)/shard_map/ppermute | solution.py:135
  21.2 10.9 %copy-start.24 = (bf16[192,256]{1,0:T(8,128)(2,1)}, bf16[192,256]{1,0:T(8,128)(2,1)S(1)}, u32[]{:S(2)}) copy-start(bf16[192,256]{1,0:T(8,128)(2,1)S(1)} %collective-permute-done.1.cross) | copy-start | bytes 294916
  21.2 7.5 %collective-permute-start.10 = (bf16[256,256]{1,0:T(8,128)(2,1)S(1)}, bf16[256,256]{1,0:T(8,128)(2,1)S(1)}, u32[]{:S(2)}, u32[]{:S(2)}) collective-permute-start(bf16[256,256]{1,0:T(8,128)(2,1)S(1)} %slice.4.refs_1_), channel_id=1, source_target_pairs={{0,64},{32,96},{64,0},{96,32},{1,65},{33,97},{65,1},{97,33},{2,66}... | collective-permute-start | bytes 393224 | tf_op jit(solution)/shard_map/ppermute | solution.py:134
  23.4 8.8 %copy-start.11 = (bf16[256,256]{1,0:T(8,128)(2,1)}, bf16[256,256]{1,0:T(8,128)(2,1)S(1)}, u32[]{:S(2)}) copy-start(bf16[256,256]{1,0:T(8,128)(2,1)S(1)} %collective-permute-done.5.refs_4_) | copy-start | bytes 393220
  23.4 7.2 %collective-permute-start.14 = (bf16[256,256]{1,0:T(8,128)(2,1)S(1)}, bf16[256,256]{1,0:T(8,128)(2,1)S(1)}, u32[]{:S(2)}, u32[]{:S(2)}) collective-permute-start(bf16[256,256]{1,0:T(8,128)(2,1)S(1)} %slice.4.refs_1_), channel_id=1, source_target_pairs={{0,32},{32,64},{64,96},{96,0},{1,33},{33,65},{65,97},{97,1},{2,34}... | collective-permute-start | bytes 393224 | tf_op jit(solution)/shard_map/ppermute | solution.py:134
  23.4 8.8 %copy-start.12 = (bf16[256,256]{1,0:T(8,128)(2,1)}, bf16[256,256]{1,0:T(8,128)(2,1)S(1)}, u32[]{:S(2)}) copy-start(bf16[256,256]{1,0:T(8,128)(2,1)S(1)} %collective-permute-done.3.refs_2_) | copy-start | bytes 393220
  23.4 7.2 %collective-permute-start.6 = (bf16[256,256]{1,0:T(8,128)(2,1)S(1)}, bf16[256,256]{1,0:T(8,128)(2,1)S(1)}, u32[]{:S(2)}, u32[]{:S(2)}) collective-permute-start(bf16[256,256]{1,0:T(8,128)(2,1)S(1)} %slice.4.refs_1_), channel_id=1, source_target_pairs={{0,96},{32,0},{64,32},{96,64},{1,97},{33,1},{65,33},{97,65},{2,98}... | collective-permute-start | bytes 393224 | tf_op jit(solution)/shard_map/ppermute | solution.py:134
  25.4 6.8 %copy-start.13 = (bf16[256,256]{1,0:T(8,128)(2,1)}, bf16[256,256]{1,0:T(8,128)(2,1)S(1)}, u32[]{:S(2)}) copy-start(bf16[256,256]{1,0:T(8,128)(2,1)S(1)} %collective-permute-done.11.refs_10_) | copy-start | bytes 393220
  25.4 5.7 %collective-permute-start.7 = (bf16[256,256]{1,0:T(8,128)(2,1)S(1)}, bf16[256,256]{1,0:T(8,128)(2,1)S(1)}, u32[]{:S(2)}, u32[]{:S(2)}) collective-permute-start(bf16[256,256]{1,0:T(8,128)(2,1)S(1)} %collective-permute-done.5.refs_4_), channel_id=1, source_target_pairs={{0,16},{16,0},{1,17},{17,1},{2,18},{18,2},{3,19},{19,3},{4,20},{20... | collective-permute-start | bytes 393224 | tf_op jit(solution)/shard_map/ppermute | solution.py:135
  25.4 6.8 %copy-start.14 = (bf16[256,256]{1,0:T(8,128)(2,1)}, bf16[256,256]{1,0:T(8,128)(2,1)S(1)}, u32[]{:S(2)}) copy-start(bf16[256,256]{1,0:T(8,128)(2,1)S(1)} %collective-permute-done.15.refs_14_) | copy-start | bytes 393220
  25.4 5.7 %collective-permute-start.4 = (bf16[256,256]{1,0:T(8,128)(2,1)S(1)}, bf16[256,256]{1,0:T(8,128)(2,1)S(1)}, u32[]{:S(2)}, u32[]{:S(2)}) collective-permute-start(bf16[256,256]{1,0:T(8,128)(2,1)S(1)} %slice.4.refs_1_), channel_id=1, source_target_pairs={{0,16},{16,0},{1,17},{17,1},{2,18},{18,2},{3,19},{19,3},{4,20},{20... | collective-permute-start | bytes 393224 | tf_op jit(solution)/shard_map/ppermute | solution.py:135
  28.7 3.5 %copy-start.15 = (bf16[256,256]{1,0:T(8,128)(2,1)}, bf16[256,256]{1,0:T(8,128)(2,1)S(1)}, u32[]{:S(2)}) copy-start(bf16[256,256]{1,0:T(8,128)(2,1)S(1)} %collective-permute-done.10.refs_9_) | copy-start | bytes 393220
  28.7 2.4 %collective-permute-start.12 = (bf16[256,256]{1,0:T(8,128)(2,1)S(1)}, bf16[256,256]{1,0:T(8,128)(2,1)S(1)}, u32[]{:S(2)}, u32[]{:S(2)}) collective-permute-start(bf16[256,256]{1,0:T(8,128)(2,1)S(1)} %collective-permute-done.10.refs_9_), channel_id=1, source_target_pairs={{0,16},{16,0},{1,17},{17,1},{2,18},{18,2},{3,19},{19,3},{4,20},{20... | collective-permute-start | bytes 393224 | tf_op jit(solution)/shard_map/ppermute | solution.py:135
  30.6 1.6 %copy-start.16 = (bf16[256,256]{1,0:T(8,128)(2,1)}, bf16[256,256]{1,0:T(8,128)(2,1)S(1)}, u32[]{:S(2)}) copy-start(bf16[256,256]{1,0:T(8,128)(2,1)S(1)} %collective-permute-done.14.refs_13_) | copy-start | bytes 393220
  30.6 1.3 %collective-permute-start.16 = (bf16[256,256]{1,0:T(8,128)(2,1)S(1)}, bf16[256,256]{1,0:T(8,128)(2,1)S(1)}, u32[]{:S(2)}, u32[]{:S(2)}) collective-permute-start(bf16[256,256]{1,0:T(8,128)(2,1)S(1)} %collective-permute-done.14.refs_13_), channel_id=1, source_target_pairs={{0,16},{16,0},{1,17},{17,1},{2,18},{18,2},{3,19},{19,3},{4,20},{20... | collective-permute-start | bytes 393224 | tf_op jit(solution)/shard_map/ppermute | solution.py:135
  30.6 1.6 %copy-start.17 = (bf16[256,256]{1,0:T(8,128)(2,1)}, bf16[256,256]{1,0:T(8,128)(2,1)S(1)}, u32[]{:S(2)}) copy-start(bf16[256,256]{1,0:T(8,128)(2,1)S(1)} %collective-permute-done.6.refs_5_) | copy-start | bytes 393220
  30.6 1.5 %collective-permute-start.8 = (bf16[256,256]{1,0:T(8,128)(2,1)S(1)}, bf16[256,256]{1,0:T(8,128)(2,1)S(1)}, u32[]{:S(2)}, u32[]{:S(2)}) collective-permute-start(bf16[256,256]{1,0:T(8,128)(2,1)S(1)} %collective-permute-done.6.refs_5_), channel_id=1, source_target_pairs={{0,16},{16,0},{1,17},{17,1},{2,18},{18,2},{3,19},{19,3},{4,20},{20... | collective-permute-start | bytes 393224 | tf_op jit(solution)/shard_map/ppermute | solution.py:135
  31.1 1.1 %copy-start.18 = (bf16[256,256]{1,0:T(8,128)(2,1)}, bf16[256,256]{1,0:T(8,128)(2,1)S(1)}, u32[]{:S(2)}) copy-start(bf16[256,256]{1,0:T(8,128)(2,1)S(1)} %collective-permute-done.7.refs_6_) | copy-start | bytes 393220
  31.1 1.1 %copy-start.19 = (bf16[256,256]{1,0:T(8,128)(2,1)}, bf16[256,256]{1,0:T(8,128)(2,1)S(1)}, u32[]{:S(2)}) copy-start(bf16[256,256]{1,0:T(8,128)(2,1)S(1)} %collective-permute-done.4.refs_3_) | copy-start | bytes 393220
  31.1 1.1 %copy-start.20 = (bf16[256,256]{1,0:T(8,128)(2,1)}, bf16[256,256]{1,0:T(8,128)(2,1)S(1)}, u32[]{:S(2)}) copy-start(bf16[256,256]{1,0:T(8,128)(2,1)S(1)} %collective-permute-done.12.refs_11_) | copy-start | bytes 393220
  31.9 0.7 copy-start.21
  32.6 0.7 copy-start.22
  37.2 18.6 %collective-permute-start.19 = (bf16[48,2048]{1,0:T(8,128)(2,1)}, bf16[48,2048]{1,0:T(8,128)(2,1)S(1)}, u32[]{:S(2)}, u32[]{:S(2)}) collective-permute-start(bf16[48,2048]{1,0:T(8,128)(2,1)} %get-tuple-element.26), channel_id=1, source_target_pairs={{0,2},{2,4},{4,6},{6,8},{8,10},{10,12},{12,14},{14,0},{1,3},{3,5},... | collective-permute-start | bytes 589832 | tf_op jit(solution)/shard_map/ppermute | solution.py:145
  39.2 16.6 %collective-permute-start.20 = (bf16[48,2048]{1,0:T(8,128)(2,1)}, bf16[48,2048]{1,0:T(8,128)(2,1)S(1)}, u32[]{:S(2)}, u32[]{:S(2)}) collective-permute-start(bf16[48,2048]{1,0:T(8,128)(2,1)} %get-tuple-element.27), channel_id=1, source_target_pairs={{0,14},{2,0},{4,2},{6,4},{8,6},{10,8},{12,10},{14,12},{1,15},{3,1}... | collective-permute-start | bytes 589832 | tf_op jit(solution)/shard_map/ppermute | solution.py:145
  43.4 11.1 %collective-permute-start.21 = (bf16[48,1024]{1,0:T(8,128)(2,1)}, bf16[48,1024]{1,0:T(8,128)(2,1)S(1)}, u32[]{:S(2)}, u32[]{:S(2)}) collective-permute-start(bf16[48,1024]{1,0:T(8,128)(2,1)} %get-tuple-element.28), channel_id=1, source_target_pairs={{0,4},{2,6},{4,8},{6,10},{8,12},{10,14},{12,0},{14,2},{1,5},{3,7},... | collective-permute-start | bytes 294920 | tf_op jit(solution)/shard_map/ppermute | solution.py:144
  43.4 12.4 %collective-permute-start.22 = (bf16[48,1024]{1,0:T(8,128)(2,1)}, bf16[48,1024]{1,0:T(8,128)(2,1)S(1)}, u32[]{:S(2)}, u32[]{:S(2)}) collective-permute-start(bf16[48,1024]{1,0:T(8,128)(2,1)} %get-tuple-element.29), channel_id=1, source_target_pairs={{0,12},{2,14},{4,0},{6,2},{8,4},{10,6},{12,8},{14,10},{1,13},{3,15... | collective-permute-start | bytes 294920 | tf_op jit(solution)/shard_map/ppermute | solution.py:144
  47.6 15.3 %collective-permute-start.17 = (bf16[48,2048]{1,0:T(8,128)(2,1)}, bf16[48,2048]{1,0:T(8,128)(2,1)S(1)}, u32[]{:S(2)}, u32[]{:S(2)}) collective-permute-start(bf16[48,2048]{1,0:T(8,128)(2,1)} %get-tuple-element.22), channel_id=1, source_target_pairs={{0,2},{2,4},{4,6},{6,8},{8,10},{10,12},{12,14},{14,0},{1,3},{3,5},... | collective-permute-start | bytes 589832 | tf_op jit(solution)/shard_map/ppermute | solution.py:146
  54.5 1.3 %copy-start.25 = (bf16[48,1024]{1,0:T(8,128)(2,1)}, bf16[48,1024]{1,0:T(8,128)(2,1)S(1)}, u32[]{:S(2)}) copy-start(bf16[48,1024]{1,0:T(8,128)(2,1)S(1)} %collective-permute-done.21.p4) | copy-start | bytes 294916
  54.5 8.3 %collective-permute-start.18 = (bf16[48,2048]{1,0:T(8,128)(2,1)}, bf16[48,2048]{1,0:T(8,128)(2,1)S(1)}, u32[]{:S(2)}, u32[]{:S(2)}) collective-permute-start(bf16[48,2048]{1,0:T(8,128)(2,1)} %get-tuple-element.23), channel_id=1, source_target_pairs={{0,14},{2,0},{4,2},{6,4},{8,6},{10,8},{12,10},{14,12},{1,15},{3,1}... | collective-permute-start | bytes 589832 | tf_op jit(solution)/shard_map/ppermute | solution.py:146
  55.8 0.6 copy-start.26
  55.8 0.7 copy-start.5
  55.8 0.8 copy-start.6
  58.7 9.9 %collective-permute-start.23 = (bf16[48,2048]{1,0:T(8,128)(2,1)}, bf16[48,2048]{1,0:T(8,128)(2,1)S(1)}, u32[]{:S(2)}, u32[]{:S(2)}) collective-permute-start(bf16[48,2048]{1,0:T(8,128)(2,1)} %get-tuple-element.30), channel_id=1, source_target_pairs={{0,4},{2,6},{4,8},{6,10},{8,12},{10,14},{12,0},{14,2},{1,5},{3,7},... | collective-permute-start | bytes 589832 | tf_op jit(solution)/shard_map/ppermute | solution.py:148
  60.4 9.4 %collective-permute-start.24 = (bf16[48,2048]{1,0:T(8,128)(2,1)}, bf16[48,2048]{1,0:T(8,128)(2,1)S(1)}, u32[]{:S(2)}, u32[]{:S(2)}) collective-permute-start(bf16[48,2048]{1,0:T(8,128)(2,1)} %get-tuple-element.31), channel_id=1, source_target_pairs={{0,12},{2,14},{4,0},{6,2},{8,4},{10,6},{12,8},{14,10},{1,13},{3,15... | collective-permute-start | bytes 589832 | tf_op jit(solution)/shard_map/ppermute | solution.py:148
  62.9 6.9 %copy-start.3 = (bf16[48,2048]{1,0:T(8,128)(2,1)}, bf16[48,2048]{1,0:T(8,128)(2,1)S(1)}, u32[]{:S(2)}) copy-start(bf16[48,2048]{1,0:T(8,128)(2,1)S(1)} %collective-permute-done.17.p1) | copy-start | bytes 589828
  62.9 6.9 %copy-start.4 = (bf16[48,2048]{1,0:T(8,128)(2,1)}, bf16[48,2048]{1,0:T(8,128)(2,1)S(1)}, u32[]{:S(2)}) copy-start(bf16[48,2048]{1,0:T(8,128)(2,1)S(1)} %collective-permute-done.18.m1) | copy-start | bytes 589828
  68.6 1.2 %copy-start.7 = (bf16[48,2048]{1,0:T(8,128)(2,1)}, bf16[48,2048]{1,0:T(8,128)(2,1)S(1)}, u32[]{:S(2)}) copy-start(bf16[48,2048]{1,0:T(8,128)(2,1)S(1)} %collective-permute-done.23.up) | copy-start | bytes 589828
  69.8 0.7 copy-start.8
  70.5 2.4 %copy-start.28 = (bf16[4096]{0:T(1024)(128)(2,1)S(1)}, bf16[4096]{0:T(1024)(128)(2,1)}, u32[]{:S(2)}) copy-start(bf16[4096]{0:T(1024)(128)(2,1)} %param.7) | copy-start | bytes 24580
  72.7 4.0 %collective-permute-start.25 = (f32[48,128]{1,0:T(8,128)}, f32[48,128]{1,0:T(8,128)S(1)}, u32[]{:S(2)}, u32[]{:S(2)}) collective-permute-start(f32[48,128]{1,0:T(8,128)} %get-tuple-element.33.near), channel_id=1, source_target_pairs={{0,128},{128,0},{1,129},{129,1},{2,130},{130,2},{3,131},{131,3},{4... | collective-permute-start | bytes 73736 | tf_op jit(solution)/shard_map/ppermute | solution.py:152
  76.7 0.6 copy-start.27
